TPU v7x, 32 devices: a whole 2x2x4 slice. The times are simulated.
32 devices in a mesh: group: 2 (over y), expert: 4 (over x, core), tensor: 4 (over z).
Axes of the slice: x: 2, y: 2, z: 4, core: 2. Of those that a mesh axis runs over, the one named last changes fastest.
Arguments:
- tokens: bfloat16 [512, 4096], P(('group', 'expert'), 'tensor'), parts along dimension 0, may hold values from -6 to 6
- w_gate: bfloat16 [8, 4096, 1536], P('expert', 'tensor'), may hold values from -0.125 to 0.125
- w_up: bfloat16 [8, 4096, 1536], P('expert', 'tensor'), may hold values from -0.125 to 0.125
- w_down: bfloat16 [8, 1536, 4096], P('expert', None, 'tensor'), may hold values from -0.15625 to 0.15625
- expert_ids: int32 [512, 8], P(('group', 'expert')), parts along dimension 0, may hold values from 0 to 7, as said below
- route_weights: float32 [512, 8], P(('group', 'expert')), parts along dimension 0, may hold values from 0.05 to 0.5
Outputs:
- mixed_out: bfloat16 [512, 4096], P(('group', 'expert'), 'tensor'), parts along dimension 0
There are 2 independent parts, one for each index of `group`. A program takes and returns all parts, laid end to end along the dimension named above; an argument that names none is the same for every part. Nothing has to cross between parts.
Inputs may be any that keep to these rules, and one draw needn't show every extreme that they name: `expert_ids`: each row names 8 different experts. In each aligned block of 64 rows no expert is named by more than 64 rows, and one expert, the same in every block of a part, is named by exactly 64 rows of every block.
All inputs are finite; a program needn't handle non-finite values.
Results may differ from a plain program's by a relative error of at most 0.0057.
Values may be sent and summed in bfloat16 or wider, within the bound.
A program may use at most 128 MiB of HBM per device.

v0:
```python
import jax
import jax.numpy as jnp
from jax import lax
from jax.sharding import PartitionSpec as P


def slot_numbers(flat_ids, experts_all):
    labels = jnp.arange(experts_all, dtype=jnp.int32)
    onehot = (flat_ids[:, None] == labels[None, :]).astype(jnp.int32)
    before = jnp.cumsum(onehot, axis=0) - onehot
    return jnp.sum(before * onehot, axis=1)


def per_device(tokens, w_gate, w_up, w_down, expert_ids, route_weights):
    n_expert = lax.axis_size("expert")
    held_experts = w_gate.shape[0]
    experts_all = held_experts * n_expert
    tok_rows = tokens.shape[0]
    col_share = tokens.shape[1]
    per_token = expert_ids.shape[1]
    capacity = min(tok_rows, 2 * tok_rows * per_token // experts_all)
    flat_ids = expert_ids.reshape(tok_rows * per_token)
    position = flat_ids * capacity + slot_numbers(flat_ids, experts_all)
    owners = jnp.arange(tok_rows * per_token, dtype=jnp.int32) // per_token
    source = jnp.full((experts_all * capacity,), -1, jnp.int32).at[position].set(owners)
    filled = (source >= 0)[:, None]
    picked_rows = jnp.where(filled, tokens[jnp.maximum(source, 0)], jnp.zeros((), tokens.dtype))
    outgoing = picked_rows.reshape(n_expert, held_experts, capacity, col_share)
    received = lax.all_to_all(outgoing, "expert", split_axis=0, concat_axis=0, tiled=True)
    gate_part = jnp.einsum("sjnd,jdf->sjnf", received, w_gate, preferred_element_type=jnp.float32)
    up_part = jnp.einsum("sjnd,jdf->sjnf", received, w_up, preferred_element_type=jnp.float32)
    gate_share = lax.psum_scatter(gate_part, "tensor", scatter_dimension=3, tiled=True)
    up_share = lax.psum_scatter(up_part, "tensor", scatter_dimension=3, tiled=True)
    hidden_share = (jax.nn.silu(gate_share) * up_share).astype(jnp.bfloat16)
    hidden = lax.all_gather(hidden_share, "tensor", axis=3, tiled=True)
    result = jnp.einsum("sjnf,jfd->sjnd", hidden, w_down, preferred_element_type=jnp.float32)
    returned = result.astype(jnp.bfloat16)
    combined = lax.all_to_all(returned, "expert", split_axis=0, concat_axis=0, tiled=True).reshape(
        experts_all * capacity, col_share
    )
    picked = combined[position].reshape(tok_rows, per_token, col_share).astype(jnp.float32)
    mixed_out = jnp.sum(picked * route_weights[:, :, None], axis=1)
    return mixed_out.astype(jnp.bfloat16)


def solution(mesh):
    in_specs = (
        P(("group", "expert"), "tensor"),
        P("expert", "tensor", None),
        P("expert", "tensor", None),
        P("expert", None, "tensor"),
        P(("group", "expert"), None),
        P(("group", "expert"), None),
    )
    out_specs = P(("group", "expert"), "tensor")
    return jax.shard_map(
        per_device, mesh=mesh, in_specs=in_specs, out_specs=out_specs, check_vma=False
    )
```

profile of v0, /device:TPU:0, one launch (start us, length us, event | category | flops | bytes accessed | tf_op | source)
XLA Modules:
  0.0 236.0 jit_solution(6427868677075579159)
XLA Ops:
  6.5 0.8 copy.16
  7.3 0.1 eq.29
  7.4 0.1 eq.25
  7.5 0.7 broadcast_multiply_fusion
  8.2 1.1 reduce-window.6
  9.4 0.2 slice_reduce_fusion
  9.7 0.1 mul.32
  9.8 0.1 fusion.22
  9.9 2.4 %scatter_custom_fusion = s32[512]{0:T(512)S(1)} fusion(s32[512]{0:T(512)S(1)} %bitcast.47, s32[512]{0:T(512)S(1)} %add_select_fusion, s32[]{:T(128)} %constant.27.clone.1), kind=kCustom, calls=%fused_computation.39 | custom fusion | bytes 2052 | tf_op jit(solution)/shard_map/scatter | solution.py:25
  12.5 2.1 gather_fusion
  14.5 0.1 broadcast_select_fusion
  14.7 18.5 %all_to_all.10 = bf16[4,2,64,1024]{3,2,1,0:T(8,128)(2,1)S(1)} all-to-all(bf16[4,2,64,1024]{3,2,1,0:T(8,128)(2,1)S(1)} %broadcast_select_fusion), channel_id=1, replica_groups=mesh['group'=2,'expert'=4,'tensor'=4] {'expert'}, dimensions={0} | all-to-all | bytes 2097152 | tf_op jit(solution)/shard_map/all_to_all | solution.py:29
  33.2 6.3 %fusion.6 = f32[4,2,64,1536]{3,2,0,1:T(8,128)} fusion(bf16[2,1024,1536]{2,1,0:T(8,128)(2,1)} %param.7, bf16[4,2,64,1024]{3,2,1,0:T(8,128)(2,1)S(1)} %all_to_all.10), kind=kOutput, calls=%fused_computation.9 | convolution fusion | flops 1610612736 | bytes 10485760 | tf_op jit(solution)/shard_map/sjnd,jdf->sjnf/dot_general | solution.py:30
  39.5 6.3 %fusion.9 = f32[4,2,64,1536]{3,2,0,1:T(8,128)} fusion(bf16[2,1024,1536]{2,1,0:T(8,128)(2,1)} %param.8, bf16[4,2,64,1024]{3,2,1,0:T(8,128)(2,1)S(1)} %all_to_all.10), kind=kOutput, calls=%fused_computation.10 | convolution fusion | flops 1610612736 | bytes 10485760 | tf_op jit(solution)/shard_map/sjnd,jdf->sjnf/dot_general | solution.py:31
  45.9 54.4 %reduce-scatter.3.cloned.1.call-done = f32[4,2,64,384]{3,2,0,1:T(8,128)} async-done(((f32[4,2,64,1536]{3,2,0,1:T(8,128)}), f32[4,2,64,384]{3,2,0,1:T(8,128)}) %reduce-scatter.3.cloned.1.call-update) | async-done | bytes 786448 | tf_op jit(solution)/shard_map/reduce_scatter | solution.py:32
  100.3 62.6 %reduce-scatter.5.cloned.1.call-done = f32[4,2,64,384]{3,2,0,1:T(8,128)} async-done(((f32[4,2,64,1536]{3,2,0,1:T(8,128)}), f32[4,2,64,384]{3,2,0,1:T(8,128)}) %reduce-scatter.5.cloned.1.call-update) | async-done | bytes 786448 | tf_op jit(solution)/shard_map/reduce_scatter | solution.py:33
  163.0 2.3 multiply_convert_fusion
  165.3 36.7 %all-gather.2.cloned.1.call-done = bf16[4,2,64,1536]{3,2,0,1:T(8,128)(2,1)} async-done(((bf16[4,2,64,384]{3,2,0,1:T(8,128)(2,1)}), bf16[4,2,64,1536]{3,2,0,1:T(8,128)(2,1)}) %all-gather.2.cloned.1.call-update) | async-done | bytes 1572880 | tf_op jit(solution)/shard_map/all_gather | solution.py:35
  202.0 5.1 %fusion.16 = bf16[4,2,64,1024]{3,2,0,1:T(8,128)(2,1)S(1)} fusion(bf16[4,2,64,1536]{3,2,0,1:T(8,128)(2,1)} %all-gather.2.cloned.1.call-done, bf16[2,1536,1024]{2,1,0:T(8,128)(2,1)} %param.9), kind=kOutput, calls=%fused_computation.14 | convolution fusion | flops 1611137024 | bytes 8912896 | tf_op jit(solution)/shard_map/sjnf,jfd->sjnd/dot_general | solution.py:36
  207.1 1.1 copy.20
  208.1 3.5 %all-to-all-start.1 = ((bf16[4,2,64,1024]{3,2,1,0:T(8,128)(2,1)}), bf16[4,2,64,1024]{3,2,1,0:T(8,128)(2,1)S(1)}, u32[]{:S(2)}, u32[]{:S(2)}) async-start(bf16[4,2,64,1024]{3,2,1,0:T(8,128)(2,1)} %copy.20), calls=%async_computation.3 | async-start | bytes 2097152 | tf_op jit(solution)/shard_map/all_to_all | solution.py:38
  211.8 14.3 %all-to-all-done.1 = bf16[4,2,64,1024]{3,2,1,0:T(8,128)(2,1)S(1)} async-done(((bf16[4,2,64,1024]{3,2,1,0:T(8,128)(2,1)}), bf16[4,2,64,1024]{3,2,1,0:T(8,128)(2,1)S(1)}, u32[]{:S(2)}, u32[]{:S(2)}) %all-to-all-start.1) | async-done | bytes 1048608 | tf_op jit(solution)/shard_map/all_to_all | solution.py:38
  226.1 2.0 gather_fusion.1
  228.1 1.4 fusion.12
  (22 shorter events, 0.5 us)
Async XLA Ops:
  6.5 6.0 %copy-start = (bf16[64,1024]{1,0:T(8,128)(2,1)S(1)}, bf16[64,1024]{1,0:T(8,128)(2,1)}, u32[]{:S(2)}) copy-start(bf16[64,1024]{1,0:T(8,128)(2,1)} %param.6) | copy-start | bytes 393220
  6.5 93.8 %reduce-scatter.3.cloned.1.call-start = ((), (), s32[]{:S(2)}) async-start(), calls=%async_computation.4 | async-start | bytes 3932160 | tf_op jit(solution)/shard_map/reduce_scatter | solution.py:32
  39.5 123.5 %reduce-scatter.5.cloned.1.call-start = ((), (), s32[]{:S(2)}) async-start(), calls=%async_computation.5 | async-start | bytes 3932160 | tf_op jit(solution)/shard_map/reduce_scatter | solution.py:33
  45.8 156.2 %all-gather.2.cloned.1.call-start = ((), (), s32[]{:S(2)}) async-start(), calls=%async_computation.6 | async-start | bytes 1966080 | tf_op jit(solution)/shard_map/all_gather | solution.py:35
  165.3 46.3 %copy-start.1 = (f32[64,8]{0,1:T(8,128)S(1)}, f32[64,8]{0,1:T(8,128)}, u32[]{:S(2)}) copy-start(f32[64,8]{0,1:T(8,128)} %param.11) | copy-start | bytes 6148
  208.1 17.9 %all-to-all-start.1 = ((bf16[4,2,64,1024]{3,2,1,0:T(8,128)(2,1)}), bf16[4,2,64,1024]{3,2,1,0:T(8,128)(2,1)S(1)}, u32[]{:S(2)}, u32[]{:S(2)}) async-start(bf16[4,2,64,1024]{3,2,1,0:T(8,128)(2,1)} %copy.20), calls=%async_computation.3 | async-start | bytes 2097152 | tf_op jit(solution)/shard_map/all_to_all | solution.py:38
Sparse Core Ops, SparseCore 0:
  39.6 60.6 reduce-scatter.2
  102.6 60.3 reduce-scatter.4
  165.4 36.5 all-gather.1
where the time goes:
time: 236 us
  waiting for transfers between devices  168 us (71%)
  blocking collectives  18.5 us (8%)
  matrix products  17.6 us (7%)
  between operations  13.2 us (6%)
  local copies, waits for them, and re-layouts  9.18 us (4%)
  other arithmetic  5.83 us (2%)
  starting transfers between devices  3.6 us (2%)
    reduce_scatter x1, waiting for transfers between devices, per_device(): lax.psum_scatter(up_part, 'tensor', scatter_dimension=3, tiled=True)  62.6 us
    reduce_scatter x1, waiting for transfers between devices, per_device(): lax.psum_scatter(gate_part, 'tensor', scatter_dimension=3, tiled=True)  54.4 us
    all_gather x1, waiting for transfers between devices, per_device(): hidden = lax.all_gather(hidden_share, 'tensor', axis=3, tiled=True)  36.7 us
    all_to_all x1, blocking collectives, per_device(): lax.all_to_all(outgoing, 'expert', split_axis=0, concat_axis=0, tiled=True)  18.5 us
    all_to_all x1, waiting for transfers between devices, per_device(): lax.all_to_all(returned, 'expert', split_axis=0, concat_axis=0, tiled=True)  14.3 us
    dot_general x1, matrix products, per_device(): jnp.einsum('sjnd,jdf->sjnf', received, w_up, preferred_element_type=jnp.f...  6.3 us
    dot_general x1, matrix products, per_device(): jnp.einsum('sjnd,jdf->sjnf', received, w_gate, preferred_element_type=jnp...  6.27 us
    dot_general x1, matrix products, per_device(): jnp.einsum('sjnf,jfd->sjnd', hidden, w_down, preferred_element_type=jnp.f...  5.06 us
  transfers between devices with their start and end apart: 4, of which 4 were waited for; matrix products, arithmetic and copies ran while one was open for 3% of the time, Pallas kernels for 0%

commit v1 on v0

--- a/solution.py
+++ b/solution.py
@@ -2,6 +2,29 @@
 import jax.numpy as jnp
 from jax import lax
 from jax.sharding import PartitionSpec as P
+
+
+def deliver_plane_over_axis(mine_x, inp):
+    dev_axis = "tensor"
+    v1 = lax.axis_index(dev_axis)
+    w2 = lax.axis_size(dev_axis)
+    vec_out, f_now, e_next = (w2, v1, mine_x.shape[3])
+    tray = tuple(((k0, (k0 + 1) % vec_out) for k0 in range(vec_out)))
+    a_next = vec_out // 2
+    samples = tuple(((k0, (k0 - 1) % vec_out) for k0 in range(vec_out)))
+    v_next = built = mine_x
+    src_i = 1
+    block_now = inp(mine_x, f_now * e_next)
+    while src_i < a_next + 1:
+        v_next = lax.ppermute(v_next, dev_axis, perm=tray)
+        if src_i < vec_out - a_next:
+            built = lax.ppermute(built, axis_name=dev_axis, perm=samples)
+            local_part = inp(built, (f_now + src_i) % vec_out * e_next)
+            block_now = block_now + local_part
+        work_now = inp(v_next, (f_now - src_i) % vec_out * e_next)
+        block_now = block_now + work_now
+        src_i = src_i + 1
+    return block_now
 
 
 def slot_numbers(flat_ids, experts_all):
@@ -32,8 +55,15 @@
     gate_share = lax.psum_scatter(gate_part, "tensor", scatter_dimension=3, tiled=True)
     up_share = lax.psum_scatter(up_part, "tensor", scatter_dimension=3, tiled=True)
     hidden_share = (jax.nn.silu(gate_share) * up_share).astype(jnp.bfloat16)
-    hidden = lax.all_gather(hidden_share, "tensor", axis=3, tiled=True)
-    result = jnp.einsum("sjnf,jfd->sjnd", hidden, w_down, preferred_element_type=jnp.float32)
+    result = deliver_plane_over_axis(
+        hidden_share,
+        lambda shard, start: jnp.einsum(
+            "sjnf,jfd->sjnd",
+            shard,
+            lax.dynamic_slice_in_dim(w_down, start, shard.shape[3], axis=1),
+            preferred_element_type=jnp.float32,
+        ),
+    )
     returned = result.astype(jnp.bfloat16)
     combined = lax.all_to_all(returned, "expert", split_axis=0, concat_axis=0, tiled=True).reshape(
         experts_all * capacity, col_share

time: 236 us -> 224 us (0.949)
  waiting for transfers between devices: 168 us -> 146 us
  starting transfers between devices: 3.6 us -> 12.9 us
    all_gather x1 -> x0, waiting for transfers between devices: 36.7 us -> none  [per_device(): hidden = lax.all_gather(hidden_share, 'tensor', axis=3, tiled=True)]
    ppermute x0 -> x3, waiting for transfers between devices: none -> 14.8 us  [the longest x2 14.8 us: deliver_plane_over_axis(): v_next = lax.ppermute(v_next, dev_axis, perm=tray)]
    ppermute x0 -> x3, starting transfers between devices: none -> 9.34 us  [the longest x2 6.39 us: deliver_plane_over_axis(): v_next = lax.ppermute(v_next, dev_axis, perm=tray)]
    dot_general x1 -> x4, matrix products: 5.06 us -> 5.75 us  [per_device(): jnp.einsum('sjnf,jfd->sjnd', shard, lax.dynamic_slice_in_dim(w_down, star...]
  transfers between devices with their start and end apart: 4 -> 6, of which waited for: 4 -> 5; matrix products, arithmetic and copies ran while one was open for 3% -> 5% of each run, Pallas kernels for 0% -> 0%
where the time goes in v1:
time: 224 us
  waiting for transfers between devices  146 us (65%)
  blocking collectives  18.5 us (8%)
  matrix products  18.3 us (8%)
  between operations  13.6 us (6%)
  starting transfers between devices  12.9 us (6%)
  local copies, waits for them, and re-layouts  9.21 us (4%)
  other arithmetic  5.23 us (2%)
    reduce_scatter x1, waiting for transfers between devices, per_device(): lax.psum_scatter(up_part, 'tensor', scatter_dimension=3, tiled=True)  62.6 us
    reduce_scatter x1, waiting for transfers between devices, per_device(): lax.psum_scatter(gate_part, 'tensor', scatter_dimension=3, tiled=True)  54.5 us
    all_to_all x1, blocking collectives, per_device(): lax.all_to_all(outgoing, 'expert', split_axis=0, concat_axis=0, tiled=True)  18.5 us
    ppermute x2, waiting for transfers between devices, deliver_plane_over_axis(): v_next = lax.ppermute(v_next, dev_axis, perm=tray)  14.8 us
    all_to_all x1, waiting for transfers between devices, per_device(): lax.all_to_all(returned, 'expert', split_axis=0, concat_axis=0, tiled=True)  14.3 us
    ppermute x2, starting transfers between devices, deliver_plane_over_axis(): v_next = lax.ppermute(v_next, dev_axis, perm=tray)  6.39 us
    dot_general x1, matrix products, per_device(): jnp.einsum('sjnd,jdf->sjnf', received, w_up, preferred_element_type=jnp.f...  6.28 us
    dot_general x1, matrix products, per_device(): jnp.einsum('sjnd,jdf->sjnf', received, w_gate, preferred_element_type=jnp...  6.24 us
  transfers between devices with their start and end apart: 6, of which 5 were waited for; matrix products, arithmetic and copies ran while one was open for 5% of the time, Pallas kernels for 0%

profile of v1, /device:TPU:0, one launch (start us, length us, event | category | flops | bytes accessed | tf_op | source)
XLA Modules:
  0.0 224.0 jit_solution(14919345677644659345)
XLA Ops:
  6.5 0.8 copy.16
  8.2 1.1 reduce-window.6
  9.9 2.4 %scatter_custom_fusion = s32[512]{0:T(512)S(1)} fusion(s32[512]{0:T(512)S(1)} %bitcast.65, s32[512]{0:T(512)S(1)} %add_select_fusion, s32[]{:T(128)} %constant.58.clone.1), kind=kCustom, calls=%fused_computation.48 | custom fusion | bytes 2052 | tf_op jit(solution)/shard_map/scatter | solution.py:48
  12.5 2.1 gather_fusion
  14.7 18.5 %all_to_all.10 = bf16[4,2,64,1024]{3,2,1,0:T(8,128)(2,1)S(1)} all-to-all(bf16[4,2,64,1024]{3,2,1,0:T(8,128)(2,1)S(1)} %broadcast_select_fusion), channel_id=1, replica_groups=mesh['group'=2,'expert'=4,'tensor'=4] {'expert'}, dimensions={0} | all-to-all | bytes 2097152 | tf_op jit(solution)/shard_map/all_to_all | solution.py:52
  33.2 6.2 %fusion.4 = f32[4,2,64,1536]{3,2,0,1:T(8,128)} fusion(bf16[2,1024,1536]{2,1,0:T(8,128)(2,1)} %param.7, bf16[4,2,64,1024]{3,2,1,0:T(8,128)(2,1)S(1)} %all_to_all.10), kind=kOutput, calls=%fused_computation.7 | convolution fusion | flops 1610612736 | bytes 10485760 | tf_op jit(solution)/shard_map/sjnd,jdf->sjnf/dot_general | solution.py:53
  39.5 6.3 %fusion.7 = f32[4,2,64,1536]{3,2,0,1:T(8,128)} fusion(bf16[2,1024,1536]{2,1,0:T(8,128)(2,1)} %param.8, bf16[4,2,64,1024]{3,2,1,0:T(8,128)(2,1)S(1)} %all_to_all.10), kind=kOutput, calls=%fused_computation.8 | convolution fusion | flops 1610612736 | bytes 10485760 | tf_op jit(solution)/shard_map/sjnd,jdf->sjnf/dot_general | solution.py:54
  45.8 54.5 %reduce-scatter.3.cloned.1.call-done = f32[4,2,64,384]{3,2,0,1:T(8,128)} async-done(((f32[4,2,64,1536]{3,2,0,1:T(8,128)}), f32[4,2,64,384]{3,2,0,1:T(8,128)}) %reduce-scatter.3.cloned.1.call-update) | async-done | bytes 786448 | tf_op jit(solution)/shard_map/reduce_scatter | solution.py:55
  100.3 62.6 %reduce-scatter.5.cloned.1.call-done = f32[4,2,64,384]{3,2,0,1:T(8,128)} async-done(((f32[4,2,64,1536]{3,2,0,1:T(8,128)}), f32[4,2,64,384]{3,2,0,1:T(8,128)}) %reduce-scatter.5.cloned.1.call-update) | async-done | bytes 786448 | tf_op jit(solution)/shard_map/reduce_scatter | solution.py:56
  163.0 1.7 multiply_convert_fusion
  164.7 0.9 collective-permute-start.1
  165.6 2.9 %collective-permute-start = (bf16[4,2,64,384]{3,2,0,1:T(8,128)(2,1)S(1)}, bf16[4,2,64,384]{3,2,0,1:T(8,128)(2,1)S(1)}, u32[]{:S(2)}, u32[]{:S(2)}) collective-permute-start(bf16[4,2,64,384]{3,2,0,1:T(8,128)(2,1)S(1)} %multiply_convert_fusion), channel_id=1, source_target_pairs={{0,3},{1,0},{2,1},{3,2},{4,7},{5,4},{6,5},{7,6},{8,11},{9,8},{10,9... | collective-permute-start | bytes 1179656 | tf_op jit(solution)/shard_map/ppermute | solution.py:21
  168.6 2.1 fusion.16
  170.7 7.9 %collective-permute-done.1 = bf16[4,2,64,384]{3,2,0,1:T(8,128)(2,1)S(1)} collective-permute-done((bf16[4,2,64,384]{3,2,0,1:T(8,128)(2,1)S(1)}, bf16[4,2,64,384]{3,2,0,1:T(8,128)(2,1)S(1)}, u32[]{:S(2)}, u32[]{:S(2)}) %collective-permute-start.1) | collective-permute-done | bytes 393248 | tf_op jit(solution)/shard_map/ppermute | solution.py:19
  178.6 5.5 %collective-permute-start.2 = (bf16[4,2,64,384]{3,2,0,1:T(8,128)(2,1)S(1)}, bf16[4,2,64,384]{3,2,0,1:T(8,128)(2,1)S(1)}, u32[]{:S(2)}, u32[]{:S(2)}) collective-permute-start(bf16[4,2,64,384]{3,2,0,1:T(8,128)(2,1)S(1)} %collective-permute-done.1), channel_id=1, source_target_pairs={{0,1},{1,2},{2,3},{3,0},{4,5},{5,6},{6,7},{7,4},{8,9},{9,10},{10,1... | collective-permute-start | bytes 1179656 | tf_op jit(solution)/shard_map/ppermute | solution.py:19
  184.1 2.1 fusion.12
  186.2 0.7 fusion.14
  187.0 6.9 %collective-permute-done.2 = bf16[4,2,64,384]{3,2,0,1:T(8,128)(2,1)S(1)} collective-permute-done((bf16[4,2,64,384]{3,2,0,1:T(8,128)(2,1)S(1)}, bf16[4,2,64,384]{3,2,0,1:T(8,128)(2,1)S(1)}, u32[]{:S(2)}, u32[]{:S(2)}) %collective-permute-start.2) | collective-permute-done | bytes 393248 | tf_op jit(solution)/shard_map/ppermute | solution.py:19
  193.9 0.8 fusion.22
  194.7 1.1 copy.20
  195.8 3.5 %all-to-all-start.1 = ((bf16[4,2,64,1024]{3,2,1,0:T(8,128)(2,1)}), bf16[4,2,64,1024]{3,2,1,0:T(8,128)(2,1)S(1)}, u32[]{:S(2)}, u32[]{:S(2)}) async-start(bf16[4,2,64,1024]{3,2,1,0:T(8,128)(2,1)} %copy.20), calls=%async_computation.3 | async-start | bytes 2097152 | tf_op jit(solution)/shard_map/all_to_all | solution.py:68
  199.4 14.3 %all-to-all-done.1 = bf16[4,2,64,1024]{3,2,1,0:T(8,128)(2,1)S(1)} async-done(((bf16[4,2,64,1024]{3,2,1,0:T(8,128)(2,1)}), bf16[4,2,64,1024]{3,2,1,0:T(8,128)(2,1)S(1)}, u32[]{:S(2)}, u32[]{:S(2)}) %all-to-all-start.1) | async-done | bytes 1048608 | tf_op jit(solution)/shard_map/all_to_all | solution.py:68
  213.7 2.0 gather_fusion.1
  215.8 1.3 fusion.10
  (33 shorter events, 1.8 us)
Async XLA Ops:
  6.5 6.0 %copy-start = (bf16[64,1024]{1,0:T(8,128)(2,1)S(1)}, bf16[64,1024]{1,0:T(8,128)(2,1)}, u32[]{:S(2)}) copy-start(bf16[64,1024]{1,0:T(8,128)(2,1)} %param.6) | copy-start | bytes 393220
  6.5 93.8 %reduce-scatter.3.cloned.1.call-start = ((), (), s32[]{:S(2)}) async-start(), calls=%async_computation.4 | async-start | bytes 3932160 | tf_op jit(solution)/shard_map/reduce_scatter | solution.py:55
  39.4 123.5 %reduce-scatter.5.cloned.1.call-start = ((), (), s32[]{:S(2)}) async-start(), calls=%async_computation.5 | async-start | bytes 3932160 | tf_op jit(solution)/shard_map/reduce_scatter | solution.py:56
  163.0 23.2 %slice-start = ((s8[6291456]{0:T(1024)(128)(4,1)}), s8[2097152]{0:T(1024)(128)(4,1)S(1)}, s32[]{:S(2)}) async-start(s8[6291456]{0:T(1024)(128)(4,1)} %bitcast.62), calls=%async_computation.6 | async-start | bytes 4194304
  164.7 13.9 %collective-permute-start.1 = (bf16[4,2,64,384]{3,2,0,1:T(8,128)(2,1)S(1)}, bf16[4,2,64,384]{3,2,0,1:T(8,128)(2,1)S(1)}, u32[]{:S(2)}, u32[]{:S(2)}) collective-permute-start(bf16[4,2,64,384]{3,2,0,1:T(8,128)(2,1)S(1)} %multiply_convert_fusion), channel_id=1, source_target_pairs={{0,1},{1,2},{2,3},{3,0},{4,5},{5,6},{6,7},{7,4},{8,9},{9,10},{10,1... | collective-permute-start | bytes 1179656 | tf_op jit(solution)/shard_map/ppermute | solution.py:19
  165.6 20.6 %slice-start.1 = ((s8[6291456]{0:T(1024)(128)(4,1)}), s8[4194304]{0:T(1024)(128)(4,1)S(1)}, s32[]{:S(2)}) async-start(s8[6291456]{0:T(1024)(128)(4,1)} %bitcast.62), calls=%async_computation.7 | async-start | bytes 8388608
  165.6 20.5 %collective-permute-start = (bf16[4,2,64,384]{3,2,0,1:T(8,128)(2,1)S(1)}, bf16[4,2,64,384]{3,2,0,1:T(8,128)(2,1)S(1)}, u32[]{:S(2)}, u32[]{:S(2)}) collective-permute-start(bf16[4,2,64,384]{3,2,0,1:T(8,128)(2,1)S(1)} %multiply_convert_fusion), channel_id=1, source_target_pairs={{0,3},{1,0},{2,1},{3,2},{4,7},{5,4},{6,5},{7,6},{8,11},{9,8},{10,9... | collective-permute-start | bytes 1179656 | tf_op jit(solution)/shard_map/ppermute | solution.py:21
  178.6 15.3 %collective-permute-start.2 = (bf16[4,2,64,384]{3,2,0,1:T(8,128)(2,1)S(1)}, bf16[4,2,64,384]{3,2,0,1:T(8,128)(2,1)S(1)}, u32[]{:S(2)}, u32[]{:S(2)}) collective-permute-start(bf16[4,2,64,384]{3,2,0,1:T(8,128)(2,1)S(1)} %collective-permute-done.1), channel_id=1, source_target_pairs={{0,1},{1,2},{2,3},{3,0},{4,5},{5,6},{6,7},{7,4},{8,9},{9,10},{10,1... | collective-permute-start | bytes 1179656 | tf_op jit(solution)/shard_map/ppermute | solution.py:19
  194.7 4.6 %copy-start.1 = (f32[64,8]{0,1:T(8,128)S(1)}, f32[64,8]{0,1:T(8,128)}, u32[]{:S(2)}) copy-start(f32[64,8]{0,1:T(8,128)} %param.11) | copy-start | bytes 6148
  195.8 17.9 %all-to-all-start.1 = ((bf16[4,2,64,1024]{3,2,1,0:T(8,128)(2,1)}), bf16[4,2,64,1024]{3,2,1,0:T(8,128)(2,1)S(1)}, u32[]{:S(2)}, u32[]{:S(2)}) async-start(bf16[4,2,64,1024]{3,2,1,0:T(8,128)(2,1)} %copy.20), calls=%async_computation.3 | async-start | bytes 2097152 | tf_op jit(solution)/shard_map/all_to_all | solution.py:68
Sparse Core Ops, SparseCore 0:
  39.6 60.7 reduce-scatter.2
  102.6 60.3 reduce-scatter.4
